TPU v7x, 128 devices: a whole 4x4x4 slice. The times are simulated.
128 devices in a mesh: expert: 16 (over y, x_hi, core), dp: 8 (over x_lo, z).
Axes of the slice: x: 4 (x_hi: 2, x_lo: 2; x = x_hi * 2 + x_lo), y: 4, z: 4, core: 2. Of those that a mesh axis runs over, the one named last changes fastest.
Arguments:
- gradient: bfloat16 [8, 1, 14336, 2048], P('dp', None, None, 'expert'), may hold values from -6 to 6
- momentum: float32 [8, 1, 14336, 2048], P('dp', None, 'expert'), may hold values from -6 to 6
- group_index: int32 [224, 32, 8, 32], P('expert'), may hold values from 0 to 4095, all different within a row
Outputs:
- momentum_next: float32 [8, 1, 14336, 2048], P('dp', None, 'expert')
- update: float32 [1, 14336, 2048], P(None, None, 'expert')
Inputs may be any that keep to these rules, and one draw needn't show every extreme that they name: `group_index`: an entry names the coefficient at row frequency (entry // 64) and column frequency (entry % 64) of its block; the 32 entries of one block and replica differ.
All inputs are finite; a program needn't handle non-finite values.
Results may differ from a plain program's by a relative error of at most 0.0003.
Values may be sent and summed in bfloat16 or wider, within the bound.
A program may use at most 192 MiB of HBM per device.

v0:
```python
import math
import jax
import jax.numpy as jnp
from jax import lax
from jax.sharding import PartitionSpec as P

SPAN = 64
MOMENTUM_DECAY = 0.999
HIGHEST_PRECISION = lax.Precision.HIGHEST


def in_blocks(x, dim, count):
    before, after = (x.shape[:dim], x.shape[dim + 1 :])
    return jnp.moveaxis(x.reshape(*before, count, -1, *after), dim, 0)


def edges_of(length, count):
    unit = 8 if length >= 8 * count else 1
    return [length // unit * k // count * unit for k in range(1, count)]


def in_order(tiles, dim):
    shape = list(tiles.shape[1:])
    shape[dim] *= tiles.shape[0]
    return jnp.moveaxis(tiles, 0, dim).reshape(shape)


def several_exchanges(x, axis, pieces, split_dim, concat_dim):
    tiles = in_blocks(x, split_dim, lax.axis_size(axis))
    split_at = max(range(1, max(2, tiles.ndim - 1)), key=lambda d: tiles.shape[d])
    outs = []
    for piece in jnp.split(tiles, edges_of(tiles.shape[split_at], pieces), axis=split_at):
        if piece.size:
            outs.append(lax.all_to_all(piece, axis, split_axis=0, concat_axis=0, tiled=True))
    return in_order(jnp.concatenate(outs, axis=split_at), concat_dim)


def cosine_table(order_size):
    frequency = jnp.arange(order_size, dtype=jnp.float32)[:, None]
    position = jnp.arange(order_size, dtype=jnp.float32)[None, :]
    weighting = jnp.where(frequency == 0, math.sqrt(1.0 / order_size), math.sqrt(2.0 / order_size))
    return weighting * jnp.cos(math.pi * (2.0 * position + 1.0) * frequency / (2.0 * order_size))


def forward(blocks, cosine):
    return jnp.einsum("ui,piqj,vj->pquv", cosine, blocks, cosine, precision=HIGHEST_PRECISION)


def inverse(coeffs, cosine):
    return jnp.einsum("ui,pquv,vj->piqj", cosine, coeffs, cosine, precision=HIGHEST_PRECISION)


def place(values, picked, total):
    count_rows = picked.shape[0]
    count_cols = picked.shape[1]
    row_ids = jnp.arange(count_rows, dtype=jnp.int32)[:, None, None]
    col_ids = jnp.arange(count_cols, dtype=jnp.int32)[None, :, None]
    empty = jnp.zeros((count_rows, count_cols, total), jnp.float32)
    return empty.at[row_ids, col_ids, picked].add(values)


def on_device(gradient, momentum, group_index):
    cosine = cosine_table(SPAN)
    replica = lax.axis_index("dp")
    shifted = several_exchanges(gradient, "expert", 2, 2, 3)
    row_count = shifted.shape[1] * shifted.shape[2]
    col_count = shifted.shape[3]
    decayed = MOMENTUM_DECAY * momentum.reshape(row_count, col_count) + shifted.reshape(
        row_count, col_count
    ).astype(jnp.float32)
    block_rows = row_count // SPAN
    block_cols = col_count // SPAN
    blocks = decayed.reshape(block_rows, SPAN, block_cols, SPAN)
    coeffs = forward(blocks, cosine).reshape(block_rows, block_cols, SPAN * SPAN)
    own = lax.dynamic_index_in_dim(group_index, replica, 2, keepdims=False)
    values = jnp.take_along_axis(coeffs, own, axis=2)
    selected = place(values, own, SPAN * SPAN).reshape(block_rows, block_cols, SPAN, SPAN)
    restored = inverse(selected, cosine).reshape(row_count, col_count)
    momentum_next = (decayed - restored).reshape(momentum.shape)
    total = lax.psum(restored, "dp")
    update = several_exchanges(total[None], "expert", 2, 2, 1)
    return (momentum_next, update)


def solution(mesh):
    placed = (
        P("dp", None, None, "expert"),
        P("dp", None, "expert", None),
        P("expert", None, None, None),
    )
    return jax.shard_map(
        on_device,
        mesh=mesh,
        in_specs=placed,
        out_specs=(P("dp", None, "expert", None), P(None, None, "expert")),
        check_vma=False,
    )
```

profile of v0, /device:TPU:1, one launch (start us, length us, event | category | flops | bytes accessed | tf_op | source)
XLA Modules:
  0.0 818.0 jit_solution(18265335012599855802)
XLA Ops:
  7.2 0.0 copy-start
  7.2 4.3 fusion.28
  11.5 8.4 %all-to-all-start = ((bf16[16,1,1,448,128]{4,3,2,1,0:T(8,128)(2,1)}), bf16[16,1,1,448,128]{4,3,2,1,0:T(8,128)(2,1)}, u32[]{:S(2)}, u32[]{:S(2)}) async-start(bf16[16,1,1,448,128]{4,3,2,1,0:T(8,128)(2,1)} %get-tuple-element.6), calls=%async_computation | async-start | bytes 3670016 | tf_op jit(solution)/shard_map/all_to_all | solution.py:34
  19.9 25.6 %all-to-all-done = bf16[16,1,1,448,128]{4,3,2,1,0:T(8,128)(2,1)} async-done(((bf16[16,1,1,448,128]{4,3,2,1,0:T(8,128)(2,1)}), bf16[16,1,1,448,128]{4,3,2,1,0:T(8,128)(2,1)}, u32[]{:S(2)}, u32[]{:S(2)}) %all-to-all-start) | async-done | bytes 1835040 | tf_op jit(solution)/shard_map/all_to_all | solution.py:34
  45.5 5.2 all-to-all-start.1
  50.7 0.0 all-reduce.2.cloned.1.call-start
  50.8 7.7 broadcast_multiply_fusion
  58.5 12.7 %mul.98 = f32[14,64,32,64]{3,2,1,0:T(8,128)} reshape(f32[1,1,896,2048]{3,2,1,0:T(8,128)} %broadcast_multiply_fusion) | data formatting | bytes 14680064 | tf_op jit(solution)/shard_map/mul | solution.py:68
  71.2 0.0 copy-done
  71.2 0.2 constant_dynamic-slice_fusion
  71.4 0.1 shift-left_or_fusion
  71.5 0.1 reshape.107
  71.7 0.0 copy-done.3
  71.7 0.1 multiply_reduce_fusion
  71.8 0.0 copy-done.2
  71.8 0.2 and_reduce_fusion
  72.1 0.1 reshape.113
  72.2 4.2 all-to-all-done.1
  76.5 6.1 convert_bitcast_fusion
  82.5 7.3 copy.28
  89.8 11.4 %reshape.106 = f32[14,64,32,64]{3,2,1,0:T(8,128)} reshape(f32[1,1,896,16,128]{4,3,2,1,0:T(8,128)} %copy.28) | data formatting | bytes 14680064 | tf_op jit(solution)/shard_map/convert_element_type | solution.py:70
  101.2 15.0 %add.64 = f32[14,64,32,64]{3,2,1,0:T(8,128)} add(f32[14,64,32,64]{3,2,1,0:T(8,128)} %mul.98, f32[14,64,32,64]{3,2,1,0:T(8,128)} %reshape.106) | non-fusion elementwise | flops 1835008 | bytes 22020096 | tf_op jit(solution)/shard_map/add | solution.py:68
  116.2 27.7 %fusion = f32[14,32,64,64]{2,3,1,0:T(8,128)S(1)} fusion(f32[14,64,32,64]{3,2,1,0:T(8,128)} %add.64, f32[64]{0:T(128)S(1)} %get-tuple-element.11, f32[64]{0:T(128)S(1)} %get-tuple-element.10), kind=kOutput, calls=%fused_computation.2 | convolution fusion | flops 1409298432 | bytes 14680576 | tf_op jit(solution)/shard_map/ui,piqj,vj->pquv/dot_general | solution.py:46
  143.9 14.9 %fusion.8 = f32[14,32,64,64]{3,2,1,0:T(8,128)} fusion(f32[14,32,64,64]{2,3,1,0:T(8,128)S(1)} %fusion, f32[64]{0:T(128)S(1)} %get-tuple-element.11, f32[64]{0:T(128)S(1)} %get-tuple-element.10), kind=kOutput, calls=%fused_computation.25 | convolution fusion | flops 1409298432 | bytes 14680576 | tf_op jit(solution)/shard_map/ui,piqj,vj->pquv/dot_general | solution.py:46
  158.8 12.9 %reshape.95 = f32[14,32,4096]{2,1,0:T(8,128)} reshape(f32[14,32,64,64]{3,2,1,0:T(8,128)} %fusion.8) | data formatting | bytes 14680064 | tf_op jit(solution)/shard_map/reshape | solution.py:74
  171.7 199.1 %gather_fusion = f32[14336]{0:T(1024)S(1)} fusion(f32[14,32,4096]{2,1,0:T(8,128)} %reshape.95, s32[14336]{0:T(1024)S(1)} %reshape.107), kind=kCustom, calls=%fused_computation | custom fusion | bytes 286720 | tf_op jit(solution)/shard_map/jit(take_along_axis)/gather | solution.py:76
  370.8 0.1 reshape.110
  370.9 0.1 and_select_fusion
  370.9 0.1 reshape.115
  371.1 78.6 %scatter_custom_fusion = f32[1835008]{0:T(1024)} fusion(s32[14336]{0:T(1024)S(1)} %reshape.113, f32[14336]{0:T(1024)S(1)} %reshape.115, f32[]{:T(128)} %constant.15.clone.1), kind=kCustom, calls=%fused_computation.11 | custom fusion | flops 14336 | bytes 7340036
  449.7 11.5 %reshape.96 = f32[14,32,64,64]{3,2,1,0:T(8,128)} reshape(f32[1835008]{0:T(1024)} %scatter_custom_fusion) | data formatting | bytes 14680064 | tf_op jit(solution)/shard_map/reshape | solution.py:77
  461.2 18.2 %fusion.6 = f32[14,32,64,64]{2,3,1,0:T(8,128)S(1)} fusion(f32[14,32,64,64]{3,2,1,0:T(8,128)} %reshape.96, f32[64]{0:T(128)S(1)} %get-tuple-element.11, f32[64]{0:T(128)S(1)} %get-tuple-element.10), kind=kOutput, calls=%fused_computation.23 | convolution fusion | flops 1409298432 | bytes 14680576 | tf_op jit(solution)/shard_map/ui,pquv,vj->piqj/dot_general | solution.py:50
  479.4 14.7 %convolution_bitcast_fusion = f32[14,64,32,64]{3,1,2,0:T(8,128)} fusion(f32[14,32,64,64]{2,3,1,0:T(8,128)S(1)} %fusion.6, f32[64]{0:T(128)S(1)} %get-tuple-element.11, f32[64]{0:T(128)S(1)} %get-tuple-element.10), kind=kOutput, calls=%fused_computation.6 | convolution fusion | flops 1409298432 | bytes 14680576 | tf_op jit(solution)/shard_map/ui,pquv,vj->piqj/dot_general | solution.py:50
  494.1 21.3 %copy.34 = f32[14,64,32,64]{3,2,1,0:T(8,128)} copy(f32[14,64,32,64]{3,1,2,0:T(8,128)} %convolution_bitcast_fusion) | data formatting | bytes 14680064 | tf_op jit(solution)/shard_map/ui,pquv,vj->piqj/transpose | solution.py:50
  515.4 12.8 %reshape_broadcast_in_dim.3 = f32[1,896,16,128]{3,2,1,0:T(8,128)} reshape(f32[14,64,32,64]{3,2,1,0:T(8,128)} %copy.34) | data formatting | bytes 14680064 | tf_op jit(solution)/shard_map/reshape;broadcast_in_dim | solution.py:14
  528.2 0.0 all-reduce.2.cloned.1.call-update
  528.2 163.8 %all-reduce.2.cloned.1.call-done = f32[16,1,896,128]{3,0,2,1:T(8,128)} async-done(((f32[16,1,896,128]{3,0,2,1:T(8,128)}), f32[16,1,896,128]{3,0,2,1:T(8,128)}) %all-reduce.2.cloned.1.call-update) | async-done | bytes 7340048 | tf_op jit(solution)/shard_map/psum | solution.py:80
  692.0 5.5 fusion.27
  697.5 2.9 copy.36
  700.4 7.3 all-to-all-start.2
  707.7 5.1 copy.37
  712.8 40.2 %all-to-all-done.2 = f32[16,1,448,128]{3,2,1,0:T(8,128)} async-done(((f32[16,1,448,128]{3,2,1,0:T(8,128)}), f32[16,1,448,128]{3,2,1,0:T(8,128)}, u32[]{:S(2)}, u32[]{:S(2)}) %all-to-all-start.2) | async-done | bytes 3670048 | tf_op jit(solution)/shard_map/all_to_all | solution.py:34
  753.0 5.3 all-to-all-start.3
  758.2 13.2 %reshape.97 = f32[1,1,896,2048]{3,2,1,0:T(8,128)} reshape(f32[14,64,32,64]{3,2,1,0:T(8,128)} %copy.34) | data formatting | bytes 14680064 | tf_op jit(solution)/shard_map/reshape | solution.py:78
  771.5 13.0 %fusion.2 = f32[1,1,896,2048]{3,2,1,0:T(8,128)} fusion(f32[1,1,896,2048]{3,2,1,0:T(8,128)} %reshape.97, f32[16,1,1,112,8,128]{5,4,3,2,1,0:T(8,128)} %get-tuple-element.4, f32[1,1,896,2048]{3,2,1,0:T(8,128)} %param.4), kind=kLoop, calls=%fused_computation.8 | loop fusion | flops 5505024 | bytes 29360128 | tf_op jit(solution)/shard_map/sub | solution.py:79
  784.5 19.2 %all-to-all-done.3 = f32[16,1,448,128]{3,2,1,0:T(8,128)} async-done(((f32[16,1,448,128]{3,2,1,0:T(8,128)}), f32[16,1,448,128]{3,2,1,0:T(8,128)}, u32[]{:S(2)}, u32[]{:S(2)}) %all-to-all-start.3) | async-done | bytes 3670048 | tf_op jit(solution)/shard_map/all_to_all | solution.py:34
  803.6 7.0 pad_maximum_fusion
  810.7 0.0 copy-done.1
  (7 shorter events, 0.1 us)
Async XLA Ops:
  7.2 64.0 %copy-start = (s32[14,32,8,32]{3,2,1,0:T(8,128)S(1)}, s32[14,32,8,32]{3,2,1,0:T(8,128)}, u32[]{:S(2)}) copy-start(s32[14,32,8,32]{3,2,1,0:T(8,128)} %param.5) | copy-start | bytes 1376260
  11.5 34.1 %all-to-all-start = ((bf16[16,1,1,448,128]{4,3,2,1,0:T(8,128)(2,1)}), bf16[16,1,1,448,128]{4,3,2,1,0:T(8,128)(2,1)}, u32[]{:S(2)}, u32[]{:S(2)}) async-start(bf16[16,1,1,448,128]{4,3,2,1,0:T(8,128)(2,1)} %get-tuple-element.6), calls=%async_computation | async-start | bytes 3670016 | tf_op jit(solution)/shard_map/all_to_all | solution.py:34
  45.5 30.9 %all-to-all-start.1 = ((bf16[16,1,1,448,128]{4,3,2,1,0:T(8,128)(2,1)}), bf16[16,1,1,448,128]{4,3,2,1,0:T(8,128)(2,1)}, u32[]{:S(2)}, u32[]{:S(2)}) async-start(bf16[16,1,1,448,128]{4,3,2,1,0:T(8,128)(2,1)} %get-tuple-element.7), calls=%async_computation.1 | async-start | bytes 3670016 | tf_op jit(solution)/shard_map/all_to_all | solution.py:34
  50.7 641.3 %all-reduce.2.cloned.1.call-start = ((), (), s32[]{:S(2)}) async-start(), calls=%async_computation.4 | async-start | bytes 14680064 | tf_op jit(solution)/shard_map/psum | solution.py:80
  58.5 13.2 %copy-start.3 = (s32[3]{0:T(128)S(1)}, s32[3]{0:T(128)}, u32[]{:S(2)}) copy-start(s32[3]{0:T(128)} %constant.54) | copy-start | bytes 40
  58.5 13.3 %copy-start.2 = (s32[3]{0:T(128)S(1)}, s32[3]{0:T(128)}, u32[]{:S(2)}) copy-start(s32[3]{0:T(128)} %constant.57) | copy-start | bytes 40
  700.4 52.6 %all-to-all-start.2 = ((f32[16,1,448,128]{3,2,1,0:T(8,128)}), f32[16,1,448,128]{3,2,1,0:T(8,128)}, u32[]{:S(2)}, u32[]{:S(2)}) async-start(f32[16,1,448,128]{3,2,1,0:T(8,128)} %copy.36), calls=%async_computation.2 | async-start | bytes 7340032 | tf_op jit(solution)/shard_map/all_to_all | solution.py:34
  753.0 50.7 %all-to-all-start.3 = ((f32[16,1,448,128]{3,2,1,0:T(8,128)}), f32[16,1,448,128]{3,2,1,0:T(8,128)}, u32[]{:S(2)}, u32[]{:S(2)}) async-start(f32[16,1,448,128]{3,2,1,0:T(8,128)} %copy.37), calls=%async_computation.3 | async-start | bytes 7340032 | tf_op jit(solution)/shard_map/all_to_all | solution.py:34
  803.6 7.0 copy-start.1
Sparse Core Ops, SparseCore 0:
  528.4 163.5 all-reduce.1
where the time goes:
time: 834 us; the launch traced here: 818 us
  local copies, waits for them, and re-layouts  321 us (38%)
  waiting for transfers between devices  253 us (30%)
  other arithmetic  128 us (15%)
  matrix products  75.5 us (9%)
  starting transfers between devices  26.2 us (3%)
  between operations  14.6 us (2%)
    gather x2, local copies, waits for them, and re-layouts, on_device(): values = jnp.take_along_axis(coeffs, own, axis=2)  199 us
    psum x1, waiting for transfers between devices, on_device(): total = lax.psum(restored, 'dp')  164 us
    all_to_all x4, waiting for transfers between devices, several_exchanges(): lax.all_to_all(piece, axis, split_axis=0, concat_axis=0, tiled=True)  89.3 us
    unnamed x5, other arithmetic  85.1 us
    dot_general x2, matrix products, forward(): jnp.einsum('ui,piqj,vj->pquv', cosine, blocks, cosine, precision=HIGHEST_...  42.6 us
    dot_general x2, matrix products, inverse(): jnp.einsum('ui,pquv,vj->piqj', cosine, coeffs, cosine, precision=HIGHEST_...  32.9 us
    all_to_all x4, starting transfers between devices, several_exchanges(): lax.all_to_all(piece, axis, split_axis=0, concat_axis=0, tiled=True)  26.1 us
    transpose x1, local copies, waits for them, and re-layouts, inverse(): jnp.einsum('ui,pquv,vj->piqj', cosine, coeffs, cosine, precision=HIGHEST_...  21.3 us
  transfers between devices with their start and end apart: 5, of which 5 were waited for; matrix products, arithmetic and copies ran while one was open for 6% of the time, Pallas kernels for 0%

commit v1 on v0

--- a/solution.py
+++ b/solution.py
@@ -77,7 +77,7 @@
     selected = place(values, own, SPAN * SPAN).reshape(block_rows, block_cols, SPAN, SPAN)
     restored = inverse(selected, cosine).reshape(row_count, col_count)
     momentum_next = (decayed - restored).reshape(momentum.shape)
-    total = lax.psum(restored, "dp")
+    total = jnp.sum(lax.all_gather(restored, "dp"), axis=0)
     update = several_exchanges(total[None], "expert", 2, 2, 1)
     return (momentum_next, update)
 

time: 834 us -> 1270 us (1.52)
  waiting for transfers between devices: 253 us -> 652 us
  other arithmetic: 128 us -> 150 us
  local copies, waits for them, and re-layouts: 321 us -> 335 us
    all_gather x0 -> x1, waiting for transfers between devices: none -> 563 us  [on_device(): total = jnp.sum(lax.all_gather(restored, 'dp'), axis=0)]
    psum x1 -> x0, waiting for transfers between devices: 164 us -> none  [on_device(): total = lax.psum(restored, 'dp')]
    reduce_sum x0 -> x1, other arithmetic: none -> 21.8 us  [on_device(): total = jnp.sum(lax.all_gather(restored, 'dp'), axis=0)]
  transfers between devices with their start and end apart: 5 -> 5, of which waited for: 5 -> 5; matrix products, arithmetic and copies ran while one was open for 6% -> 4% of each run, Pallas kernels for 0% -> 0%
where the time goes in v1:
time: 1270 us; the launch traced here: 1250 us
  waiting for transfers between devices  652 us (51%)
  local copies, waits for them, and re-layouts  335 us (26%)
  other arithmetic  150 us (12%)
  matrix products  75.4 us (6%)
  starting transfers between devices  26.2 us (2%)
  between operations  14.7 us (1%)
    all_gather x1, waiting for transfers between devices, on_device(): total = jnp.sum(lax.all_gather(restored, 'dp'), axis=0)  563 us
    gather x2, local copies, waits for them, and re-layouts, on_device(): values = jnp.take_along_axis(coeffs, own, axis=2)  199 us
    all_to_all x4, waiting for transfers between devices, several_exchanges(): lax.all_to_all(piece, axis, split_axis=0, concat_axis=0, tiled=True)  89.1 us
    unnamed x5, other arithmetic  85.1 us
    dot_general x2, matrix products, forward(): jnp.einsum('ui,piqj,vj->pquv', cosine, blocks, cosine, precision=HIGHEST_...  42.6 us
    dot_general x2, matrix products, inverse(): jnp.einsum('ui,pquv,vj->piqj', cosine, coeffs, cosine, precision=HIGHEST_...  32.8 us
    all_to_all x4, starting transfers between devices, several_exchanges(): lax.all_to_all(piece, axis, split_axis=0, concat_axis=0, tiled=True)  26.1 us
  transfers between devices with their start and end apart: 5, of which 5 were waited for; matrix products, arithmetic and copies ran while one was open for 4% of the time, Pallas kernels for 0%

profile of v1, /device:TPU:1, one launch (start us, length us, event | category | flops | bytes accessed | tf_op | source)
XLA Modules:
  0.0 1253.3 jit_solution(15264112155570038276)
XLA Ops:
  7.2 0.0 copy-start
  7.2 0.0 copy-start.3
  7.2 0.0 copy-start.2
  7.2 4.3 fusion.28
  11.5 8.4 all-to-all-start
  19.9 25.6 %all-to-all-done = bf16[16,1,1,448,128]{4,3,2,1,0:T(8,128)(2,1)} async-done(((bf16[16,1,1,448,128]{4,3,2,1,0:T(8,128)(2,1)}), bf16[16,1,1,448,128]{4,3,2,1,0:T(8,128)(2,1)}, u32[]{:S(2)}, u32[]{:S(2)}) %all-to-all-start) | async-done | bytes 1835040 | tf_op jit(solution)/shard_map/all_to_all | solution.py:34
  45.5 5.2 all-to-all-start.1
  50.7 0.0 all-gather.2.cloned.1.call-start
  50.8 0.2 constant_dynamic-slice_fusion
  51.0 0.1 shift-left_or_fusion
  51.1 0.1 reshape.103
  51.3 0.1 multiply_reduce_fusion
  51.4 0.2 and_reduce_fusion
  51.7 0.1 reshape.109
  51.8 7.7 broadcast_multiply_fusion
  59.5 12.7 %mul.98 = f32[14,64,32,64]{3,2,1,0:T(8,128)} reshape(f32[1,1,896,2048]{3,2,1,0:T(8,128)} %broadcast_multiply_fusion) | data formatting | bytes 14680064 | tf_op jit(solution)/shard_map/mul | solution.py:68
  72.2 4.3 all-to-all-done.1
  76.5 6.1 convert_bitcast_fusion
  82.5 7.3 copy.28
  89.8 11.4 reshape.102
  101.2 15.0 %add.62 = f32[14,64,32,64]{3,2,1,0:T(8,128)} add(f32[14,64,32,64]{3,2,1,0:T(8,128)} %mul.98, f32[14,64,32,64]{3,2,1,0:T(8,128)} %reshape.102) | non-fusion elementwise | flops 1835008 | bytes 22020096 | tf_op jit(solution)/shard_map/add | solution.py:68
  116.2 27.7 %fusion = f32[14,32,64,64]{2,3,1,0:T(8,128)S(1)} fusion(f32[14,64,32,64]{3,2,1,0:T(8,128)} %add.62, f32[64]{0:T(128)S(1)} %get-tuple-element.11, f32[64]{0:T(128)S(1)} %get-tuple-element.10), kind=kOutput, calls=%fused_computation.2 | convolution fusion | flops 1409298432 | bytes 14680576 | tf_op jit(solution)/shard_map/ui,piqj,vj->pquv/dot_general | solution.py:46
  144.0 14.9 %fusion.8 = f32[14,32,64,64]{3,2,1,0:T(8,128)} fusion(f32[14,32,64,64]{2,3,1,0:T(8,128)S(1)} %fusion, f32[64]{0:T(128)S(1)} %get-tuple-element.11, f32[64]{0:T(128)S(1)} %get-tuple-element.10), kind=kOutput, calls=%fused_computation.25 | convolution fusion | flops 1409298432 | bytes 14680576 | tf_op jit(solution)/shard_map/ui,piqj,vj->pquv/dot_general | solution.py:46
  158.8 12.9 %reshape.93 = f32[14,32,4096]{2,1,0:T(8,128)} reshape(f32[14,32,64,64]{3,2,1,0:T(8,128)} %fusion.8) | data formatting | bytes 14680064 | tf_op jit(solution)/shard_map/reshape | solution.py:74
  171.7 199.3 %gather_fusion = f32[14336]{0:T(1024)S(1)} fusion(f32[14,32,4096]{2,1,0:T(8,128)} %reshape.93, s32[14336]{0:T(1024)S(1)} %reshape.103), kind=kCustom, calls=%fused_computation | custom fusion | bytes 286720 | tf_op jit(solution)/shard_map/jit(take_along_axis)/gather | solution.py:76
  371.1 0.1 reshape.106
  371.2 0.1 and_select_fusion
  371.2 0.1 reshape.111
  371.4 78.6 %scatter_custom_fusion = f32[1835008]{0:T(1024)} fusion(s32[14336]{0:T(1024)S(1)} %reshape.109, f32[14336]{0:T(1024)S(1)} %reshape.111, f32[]{:T(128)} %constant.15.clone.1), kind=kCustom, calls=%fused_computation.11 | custom fusion | flops 14336 | bytes 7340036
  450.0 11.5 reshape.94
  461.5 18.2 %fusion.6 = f32[14,32,64,64]{2,3,1,0:T(8,128)S(1)} fusion(f32[14,32,64,64]{3,2,1,0:T(8,128)} %reshape.94, f32[64]{0:T(128)S(1)} %get-tuple-element.11, f32[64]{0:T(128)S(1)} %get-tuple-element.10), kind=kOutput, calls=%fused_computation.23 | convolution fusion | flops 1409298432 | bytes 14680576 | tf_op jit(solution)/shard_map/ui,pquv,vj->piqj/dot_general | solution.py:50
  479.7 14.6 %convolution_bitcast_fusion = f32[14,64,32,64]{3,1,2,0:T(8,128)} fusion(f32[14,32,64,64]{2,3,1,0:T(8,128)S(1)} %fusion.6, f32[64]{0:T(128)S(1)} %get-tuple-element.11, f32[64]{0:T(128)S(1)} %get-tuple-element.10), kind=kOutput, calls=%fused_computation.6 | convolution fusion | flops 1409298432 | bytes 14680576 | tf_op jit(solution)/shard_map/ui,pquv,vj->piqj/dot_general | solution.py:50
  494.4 21.3 %copy.34 = f32[14,64,32,64]{3,2,1,0:T(8,128)} copy(f32[14,64,32,64]{3,1,2,0:T(8,128)} %convolution_bitcast_fusion) | data formatting | bytes 14680064 | tf_op jit(solution)/shard_map/ui,pquv,vj->piqj/transpose | solution.py:50
  515.7 13.5 %all_gather_reshape.3 = f32[1,896,2048]{2,1,0:T(8,128)} reshape(f32[14,64,32,64]{3,2,1,0:T(8,128)} %copy.34) | data formatting | bytes 14680064 | tf_op jit(solution)/shard_map/all_gather;reshape | solution.py:80
  529.2 0.0 all-gather.2.cloned.1.call-update
  529.2 562.8 %all-gather.2.cloned.1.call-done = f32[8,896,2048]{2,1,0:T(8,128)} async-done(((f32[1,896,2048]{2,1,0:T(8,128)}), f32[8,896,2048]{2,1,0:T(8,128)}) %all-gather.2.cloned.1.call-update) | async-done | bytes 58720272 | tf_op jit(solution)/shard_map/all_gather | solution.py:80
  1092.0 21.8 %reduce_sum.9 = f32[896,2048]{1,0:T(8,128)} reduce(f32[8,896,2048]{2,1,0:T(8,128)} %all-gather.2.cloned.1.call-done, f32[]{:T(128)} %constant.15.clone.1), dimensions={0}, to_apply=%region_1.2 | reduce | flops 12845056 | bytes 66060292 | tf_op jit(solution)/shard_map/reduce_sum | solution.py:80
  1113.8 8.6 copy.36
  1122.3 8.1 fusion.27
  1130.4 5.3 copy.37
  1135.7 7.3 all-to-all-start.2
  1143.0 5.3 copy.38
  1148.3 40.0 %all-to-all-done.2 = f32[16,1,448,128]{3,2,1,0:T(8,128)} async-done(((f32[16,1,448,128]{3,2,1,0:T(8,128)}), f32[16,1,448,128]{3,2,1,0:T(8,128)}, u32[]{:S(2)}, u32[]{:S(2)}) %all-to-all-start.2) | async-done | bytes 3670048 | tf_op jit(solution)/shard_map/all_to_all | solution.py:34
  1188.3 5.3 all-to-all-start.3
  1193.6 13.2 %reshape.95 = f32[1,1,896,2048]{3,2,1,0:T(8,128)} reshape(f32[14,64,32,64]{3,2,1,0:T(8,128)} %copy.34) | data formatting | bytes 14680064 | tf_op jit(solution)/shard_map/reshape | solution.py:78
  1206.8 13.0 %fusion.2 = f32[1,1,896,2048]{3,2,1,0:T(8,128)} fusion(f32[1,1,896,2048]{3,2,1,0:T(8,128)} %reshape.95, f32[16,1,1,112,8,128]{5,4,3,2,1,0:T(8,128)} %get-tuple-element.4, f32[1,1,896,2048]{3,2,1,0:T(8,128)} %param.4), kind=kLoop, calls=%fused_computation.8 | loop fusion | flops 5505024 | bytes 29360128 | tf_op jit(solution)/shard_map/sub | solution.py:79
  1219.8 19.2 %all-to-all-done.3 = f32[16,1,448,128]{3,2,1,0:T(8,128)} async-done(((f32[16,1,448,128]{3,2,1,0:T(8,128)}), f32[16,1,448,128]{3,2,1,0:T(8,128)}, u32[]{:S(2)}, u32[]{:S(2)}) %all-to-all-start.3) | async-done | bytes 3670048 | tf_op jit(solution)/shard_map/all_to_all | solution.py:34
  1239.0 7.0 pad_maximum_fusion
  (9 shorter events, 0.1 us)
Async XLA Ops:
  7.2 43.6 %copy-start = (s32[14,32,8,32]{3,2,1,0:T(8,128)S(1)}, s32[14,32,8,32]{3,2,1,0:T(8,128)}, u32[]{:S(2)}) copy-start(s32[14,32,8,32]{3,2,1,0:T(8,128)} %param.5) | copy-start | bytes 1376260
  7.2 44.1 %copy-start.3 = (s32[3]{0:T(128)S(1)}, s32[3]{0:T(128)}, u32[]{:S(2)}) copy-start(s32[3]{0:T(128)} %constant.55) | copy-start | bytes 40
  7.2 44.2 %copy-start.2 = (s32[3]{0:T(128)S(1)}, s32[3]{0:T(128)}, u32[]{:S(2)}) copy-start(s32[3]{0:T(128)} %constant.58) | copy-start | bytes 40
  11.5 34.1 %all-to-all-start = ((bf16[16,1,1,448,128]{4,3,2,1,0:T(8,128)(2,1)}), bf16[16,1,1,448,128]{4,3,2,1,0:T(8,128)(2,1)}, u32[]{:S(2)}, u32[]{:S(2)}) async-start(bf16[16,1,1,448,128]{4,3,2,1,0:T(8,128)(2,1)} %get-tuple-element.6), calls=%async_computation | async-start | bytes 3670016 | tf_op jit(solution)/shard_map/all_to_all | solution.py:34
  45.5 30.9 %all-to-all-start.1 = ((bf16[16,1,1,448,128]{4,3,2,1,0:T(8,128)(2,1)}), bf16[16,1,1,448,128]{4,3,2,1,0:T(8,128)(2,1)}, u32[]{:S(2)}, u32[]{:S(2)}) async-start(bf16[16,1,1,448,128]{4,3,2,1,0:T(8,128)(2,1)} %get-tuple-element.7), calls=%async_computation.1 | async-start | bytes 3670016 | tf_op jit(solution)/shard_map/all_to_all | solution.py:34
  50.7 1041.2 %all-gather.2.cloned.1.call-start = ((), (), s32[]{:S(2)}) async-start(), calls=%async_computation.4 | async-start | bytes 66060288 | tf_op jit(solution)/shard_map/all_gather | solution.py:80
  1135.7 52.6 %all-to-all-start.2 = ((f32[16,1,448,128]{3,2,1,0:T(8,128)}), f32[16,1,448,128]{3,2,1,0:T(8,128)}, u32[]{:S(2)}, u32[]{:S(2)}) async-start(f32[16,1,448,128]{3,2,1,0:T(8,128)} %copy.37), calls=%async_computation.2 | async-start | bytes 7340032 | tf_op jit(solution)/shard_map/all_to_all | solution.py:34
  1188.3 50.7 %all-to-all-start.3 = ((f32[16,1,448,128]{3,2,1,0:T(8,128)}), f32[16,1,448,128]{3,2,1,0:T(8,128)}, u32[]{:S(2)}, u32[]{:S(2)}) async-start(f32[16,1,448,128]{3,2,1,0:T(8,128)} %copy.38), calls=%async_computation.3 | async-start | bytes 7340032 | tf_op jit(solution)/shard_map/all_to_all | solution.py:34
  1239.0 7.0 copy-start.1
Sparse Core Ops, SparseCore 0:
  529.3 562.5 all-gather.1
